TPU v7x, 32 devices: a whole 2x2x4 slice. The times are simulated.
32 devices in a mesh: pgroup: 8 (over y, x, core), tile: 4 (over z).
Axes of the slice: x: 2, y: 2, z: 4, core: 2. Of those that a mesh axis runs over, the one named last changes fastest.
Arguments:
- images: float32 [64, 256, 2048], P(('pgroup', 'tile')), may hold values from -6 to 6
- beams: float32 [64, 256, 2048], P(('pgroup', 'tile')), may hold values from 0.2 to 1
- row_block: int32 [64], P(('pgroup', 'tile')), may hold values from 0 to 14, as said below
- col_block: int32 [64], P(('pgroup', 'tile')), may hold values from 0 to 16
- band: int32 [64, 2], P(('pgroup', 'tile')), may hold values from 0 to 3
- row_frac: float32 [64], P(('pgroup', 'tile')), may hold values from 0.05 to 0.95
- col_frac: float32 [64], P(('pgroup', 'tile')), may hold values from 0.05 to 0.95
Outputs:
- numer: float32 [2048, 4096], P('tile', 'pgroup')
- weight: float32 [2048, 4096], P('tile', 'pgroup')
- normalised: float32 [2048, 4096], P('tile', 'pgroup')
Inputs may be any that keep to these rules, and one draw needn't show every extreme that they name: With t = (p // 2) mod 4, row_block[p] - 4 t lies in 0 to 2, and the largest value is taken in every draw.
All inputs are finite; a program needn't handle non-finite values.
Results may differ from a plain program's by a relative error of at most 0.00002.
Values sent between devices are 32-bit elements; how exact they have to be, the bound alone decides.
A program may use at most 128 MiB of HBM per device.

v0:
```python
import functools
import math

import jax
import jax.numpy as jnp
from jax import lax
from jax.experimental import pallas as pl
from jax.experimental.pallas import tpu as pltpu
from jax.sharding import PartitionSpec as P

TILE_BLOCKS = 4
SKY_COLS = 4096
HALO = 4
LANES = 128
BLOCK = 128
ROWS = 32
PER_BLOCK = BLOCK // (2 * ROWS)
TALL = BLOCK + 8
AHEAD = 1
LAG = 2
MESH = pl.DeviceIdType.MESH
F32 = jnp.float32


def chip_grid(groups):
    chips = groups // 2
    along_x = math.isqrt(chips)
    while chips % along_x:
        along_x -= 1
    return chips // along_x, along_x


def kernel(
    ny, nx, n_tile,
    images, beams, row_block, col_block, band, row_frac, col_frac,
    out,
    raw, mid, placed, halo_out, halo_in, give, take, canvas,
    first_a, first_b, second_a, second_b, last,
    ready,
    load_sem, halo_sem, swap_sem, first_sem, second_sem, last_sem, out_sem,
):
    points, img_rows, width = images.shape
    blocks = img_rows // BLOCK
    col_tiles = width // LANES
    sky_tiles = SKY_COLS // LANES
    own = sky_tiles // (ny * nx)
    half = own // 2
    pairs = TILE_BLOCKS * PER_BLOCK
    per_array = points * blocks * col_tiles
    empty = 2 * per_array

    me = lax.axis_index("pgroup")
    tile = lax.axis_index("tile")
    core = lax.rem(me, 2)
    chip = me // 2
    x = lax.rem(chip, nx)
    y = chip // nx
    partner = me + 1 - 2 * core
    x_peers = [(y * nx + lax.rem(x + d, nx)) * 2 + core for d in range(1, nx)]
    y_peers = [(lax.rem(y + d, ny) * nx + x) * 2 + core for d in range(1, ny)]
    after = lax.rem(tile + 1, n_tile)
    before = lax.rem(tile + n_tile - 1, n_tile)

    loads = {}
    for b in reversed(range(blocks)):
        for p in range(points):
            for which, source in enumerate((images, beams)):
                rows = pl.ds(b * BLOCK, BLOCK)
                copy = pltpu.make_async_copy(
                    source.at[p, rows], raw.at[which, p, rows], load_sem.at[which, p * blocks + b]
                )
                copy.start()
                loads[which, p, b] = copy

    barrier = pltpu.get_barrier_semaphore()
    near = [{"pgroup": q} for q in [partner] + x_peers + y_peers]
    near += [{"tile": after}, {"tile": before}]
    for device in near:
        pl.semaphore_signal(barrier, inc=1, device_id=device, device_id_type=MESH)

    placed[empty] = jnp.zeros((TALL, LANES), F32)
    for slot in range(4):
        mid[slot, :8] = jnp.zeros((8, LANES), F32)
        mid[slot, 8 + BLOCK :] = jnp.zeros((8, LANES), F32)
    last_lane = lax.broadcasted_iota(jnp.int32, (BLOCK, LANES), 1) == LANES - 1

    def interpolate(a, fresh, some):
        for b in some:
            for p in range(points):
                f = row_frac[p]
                g = col_frac[p]
                if fresh:
                    loads[0, p, b].wait()
                    loads[1, p, b].wait()
                shift = band[p, b]
                rows = pl.ds(b * BLOCK, BLOCK)

                def some_tiles(step, _, p=p, b=b, f=f, g=g, shift=shift, rows=rows):
                    for sub in range(4):
                        t = 4 * step + sub
                        lanes = pl.ds(pl.multiple_of(t * LANES, LANES), LANES)
                        here = raw[1, p, rows, lanes] * raw[a, p, rows, lanes]
                        if sub == 0:
                            left = pl.ds(pl.multiple_of(jnp.maximum(t - 1, 0) * LANES, LANES), LANES)
                            there = jnp.where(t > 0, 1.0, 0.0)
                            prior = raw[1, p, rows, left] * raw[a, p, rows, left] * there
                        else:
                            left = pl.ds(pl.multiple_of((t - 1) * LANES, LANES), LANES)
                            prior = raw[1, p, rows, left] * raw[a, p, rows, left]
                        moved = pltpu.roll(jnp.where(last_lane, prior, here), 1, 1)
                        mid[sub, 8 : 8 + BLOCK] = (1.0 - g) * here + g * moved
                        low = mid[sub, pl.ds(8 - shift, TALL)]
                        high = mid[sub, pl.ds(7 - shift, TALL)]
                        index = a * per_array + (p * blocks + b) * col_tiles + t
                        placed[index] = (1.0 - f) * low + f * high
                    return 0

                lax.fori_loop(0, col_tiles // 4, some_tiles, 0)

    def where_placed(a, p, sky_block, sky_tile):
        b = sky_block - (row_block[p] - tile * TILE_BLOCKS)
        t = sky_tile - col_block[p]
        inside = (b >= 0) & (b < blocks) & (t >= 0) & (t < col_tiles)
        index = a * per_array + (p * blocks + b) * col_tiles + t
        return jnp.where(inside, index, empty)

    def slot_of(sky_tile, x_major):
        if not x_major:
            return sky_tile
        owner = sky_tile // own
        return (lax.rem(owner, nx) * ny + owner // nx) * own + lax.rem(sky_tile, own)

    def place_of(m, lower):
        m = jnp.int32(m)
        sky_block = TILE_BLOCKS - 1 - m // PER_BLOCK
        turn = lax.rem(m, PER_BLOCK)
        start = BLOCK - ROWS * (2 * turn + (1 if lower else 2))
        return sky_block, pl.multiple_of(start, ROWS)

    def gather(a, m, sky_tile, lower):
        sky_block, start = place_of(m, lower)
        total = None
        for p in range(points):
            term = placed[where_placed(a, p, sky_block, sky_tile), pl.ds(start, ROWS)]
            total = term if total is None else total + term
        if lower:
            return total, None
        top = total[:8]
        for p in range(points):
            index = jnp.where(start == 0, where_placed(a, p, sky_block - 1, sky_tile), empty)
            top = top + placed[index, BLOCK:TALL]
        return total, top

    def border(sky_tile, _):
        for a in range(2):
            top = None
            for p in range(points):
                term = placed[where_placed(a, p, TILE_BLOCKS - 1, sky_tile), BLOCK:TALL]
                top = term if top is None else top + term
            halo_out[a, sky_tile] = top
        return 0

    halo = pltpu.make_async_remote_copy(
        halo_out, halo_in, halo_sem.at[0], halo_sem.at[1],
        device_id={"tile": after}, device_id_type=MESH,
    )

    def swap(k):
        return pltpu.make_async_remote_copy(
            give.at[k], take.at[k], swap_sem.at[0, k], swap_sem.at[1, k],
            device_id={"pgroup": partner}, device_id_type=MESH,
        )

    def build(k, j, lower):
        other = 1 - core

        def one(sky_tile, _):
            total, top = gather(other, j, sky_tile, lower)
            slot = slot_of(sky_tile, lower)
            give[k, slot] = total
            if top is not None:
                give[k, slot, :8] = top
            return 0

        lax.fori_loop(0, sky_tiles, one, 0, unroll=2)
        if not lower:
            @pl.when(jnp.int32(j) == pairs - 1)
            def _():
                halo.wait_recv()
                use = jnp.where(tile > 0, 1.0, 0.0)

                def add(s, _):
                    give[k, s, :8] += use * halo_in[other, s]
                    return 0

                lax.fori_loop(0, sky_tiles, add, 0, unroll=4)
        swap(k).start()

    def first_copies(k, j, lower):
        copies = []
        count, at, peers = (nx, x, x_peers) if lower else (ny, y, y_peers)
        size = sky_tiles // count
        target = first_a if lower else first_b
        for d in range(1, count):
            to = lax.rem(at + d, count)
            copies.append(pltpu.make_async_remote_copy(
                canvas.at[k, pl.ds(to * size, size)], target.at[j, d - 1],
                first_sem.at[0, k, d - 1], first_sem.at[1, k, d - 1],
                device_id={"pgroup": peers[d - 1]}, device_id_type=MESH,
            ))
        return copies

    def second_copies(k, j, lower):
        copies = []
        count, at, peers = (ny, y, y_peers) if lower else (nx, x, x_peers)
        base = (x * ny if lower else y * nx) * own
        target = second_a if lower else second_b
        for d in range(1, count):
            to = lax.rem(at + d, count)
            copies.append(pltpu.make_async_remote_copy(
                canvas.at[k, pl.ds(base + to * own, own)], target.at[j, d - 1],
                second_sem.at[0, k, d - 1], second_sem.at[1, k, d - 1],
                device_id={"pgroup": peers[d - 1]}, device_id_type=MESH,
            ))
        return copies

    def combine(k, j, lower):
        swap(k).wait_recv()

        def one(sky_tile, _):
            total, top = gather(core, j, sky_tile, lower)
            slot = slot_of(sky_tile, lower)
            canvas[k, slot] = total + take[k, slot]
            if top is not None:
                canvas[k, slot, :8] = top + take[k, slot, :8]
            return 0

        lax.fori_loop(0, sky_tiles, one, 0, unroll=2)
        if not lower:
            @pl.when(jnp.int32(j) == pairs - 1)
            def _():
                use = jnp.where(tile > 0, 1.0, 0.0)

                def add(s, _):
                    canvas[k, s, :8] += use * halo_in[core, s]
                    return 0

                lax.fori_loop(0, sky_tiles, add, 0, unroll=4)
        for copy in first_copies(k, j, lower):
            copy.start()

    groups = [[blocks - 1], list(reversed(range(blocks - 1)))]
    interpolate(1 - core, True, groups[0])
    pl.semaphore_wait(barrier, len(near))
    build(0, 0, True)
    build(1, 0, False)
    interpolate(core, False, groups[0])
    combine(0, 0, True)
    combine(1, 0, False)
    interpolate(1 - core, True, groups[1])
    for m in range(1, 1 + AHEAD):
        build(2 * m, m, True)
        build(2 * m + 1, m, False)
    interpolate(core, False, groups[1])

    def spread(j, _):
        for lower in (True, False):
            combine(2 * j + (0 if lower else 1), j, lower)

        @pl.when(j == 1)
        def _():
            lax.fori_loop(0, sky_tiles, border, 0)
            halo.start()

        @pl.when(j < pairs - AHEAD)
        def _():
            for lower in (True, False):
                build(2 * (j + AHEAD) + (0 if lower else 1), j + AHEAD, lower)
        return 0

    lax.fori_loop(1, pairs, spread, 0)

    def middle(j, _):
        for lower in (True, False):
            k = 2 * j + (0 if lower else 1)
            copies = first_copies(k, j, lower)
            for copy in copies:
                copy.wait_recv()
            count, at = (nx, x) if lower else (ny, y)
            size = sky_tiles // count
            source = first_a if lower else first_b

            def one(s, _):
                total = canvas[k, at * size + s]
                for d in range(count - 1):
                    total = total + source[j, d, s]
                canvas[k, at * size + s] = total
                return 0

            lax.fori_loop(0, size, one, 0, unroll=2)
            for copy in second_copies(k, j, lower):
                copy.start()
            swap(k).wait_send()
        return 0

    lax.fori_loop(0, pairs, middle, 0)

    def mine(lower):
        return (x * ny + y if lower else y * nx + x) * own

    def last_copy(k, lower):
        return pltpu.make_async_remote_copy(
            canvas.at[k, pl.ds(mine(lower) + (1 - core) * half, half)], last.at[k],
            last_sem.at[0, k], last_sem.at[1, k],
            device_id={"pgroup": partner}, device_id_type=MESH,
        )

    def rows_of(j, lower):
        sky_block, start = place_of(j, lower)
        return pl.ds(pl.multiple_of(sky_block * BLOCK + start, ROWS), ROWS)

    def store(k, j, lower, a):
        rows = rows_of(j, lower)
        return pltpu.make_async_copy(ready.at[a, rows], out.at[a, rows], out_sem.at[a, k])

    def finish(j, _):
        for lower in (True, False):
            k = 2 * j + (0 if lower else 1)
            for copy in second_copies(k, j, lower):
                copy.wait_recv()
            source = second_a if lower else second_b
            count = ny if lower else nx
            rows = rows_of(j, lower)

            def summed(s):
                total = canvas[k, mine(lower) + s]
                for d in range(count - 1):
                    total = total + source[j, d, s]
                return total

            for s in range(half):
                canvas[k, mine(lower) + (1 - core) * half + s] = summed((1 - core) * half + s)
            last_copy(k, lower).start()
            for s in range(half):
                ready[core, rows, s * LANES : (s + 1) * LANES] = summed(core * half + s)
            store(k, j, lower, core).start()
            for copy in first_copies(k, j, lower):
                copy.wait_send()

        @pl.when(j >= LAG)
        def _():
            receive(j - LAG, 0)

        return 0

    def receive(j, _):
        for lower in (True, False):
            k = 2 * j + (0 if lower else 1)
            last_copy(k, lower).wait()
            rows = rows_of(j, lower)
            for s in range(half):
                ready[1 - core, rows, s * LANES : (s + 1) * LANES] = last[k, s]
            store(k, j, lower, 1 - core).start()
            for copy in second_copies(k, j, lower):
                copy.wait_send()
        return 0

    lax.fori_loop(0, pairs, finish, 0)
    lax.fori_loop(pairs - LAG, pairs, receive, 0)

    def stored(j, _):
        for lower in (True, False):
            for a in (core, 1 - core):
                store(2 * j + (0 if lower else 1), j, lower, a).wait()
        return 0

    lax.fori_loop(0, pairs, stored, 0)
    halo.wait_send()


def body(ny, nx, n_tile, images, beams, row_block, col_block, band, row_frac, col_frac):
    points, img_rows, width = images.shape
    blocks = img_rows // BLOCK
    col_tiles = width // LANES
    sky_tiles = SKY_COLS // LANES
    own = sky_tiles // (ny * nx)
    pairs = TILE_BLOCKS * PER_BLOCK
    chunks = 2 * pairs
    own_cols = SKY_COLS // (2 * ny * nx)
    most = max(nx, ny) - 1
    dma = pltpu.SemaphoreType.DMA
    smem = pl.BlockSpec(memory_space=pltpu.SMEM)
    summed = pl.pallas_call(
        functools.partial(kernel, ny, nx, n_tile),
        out_shape=jax.ShapeDtypeStruct((2, TILE_BLOCKS * BLOCK, own_cols), F32),
        in_specs=[pl.BlockSpec(memory_space=pl.ANY)] * 2 + [smem] * 5,
        out_specs=pl.BlockSpec(memory_space=pl.ANY),
        scratch_shapes=[
            pltpu.VMEM((2, points, img_rows, width), F32),
            pltpu.VMEM((4, BLOCK + 16, LANES), F32),
            pltpu.VMEM((2 * points * blocks * col_tiles + 1, TALL, LANES), F32),
            pltpu.VMEM((2, sky_tiles, 8, LANES), F32),
            pltpu.VMEM((2, sky_tiles, 8, LANES), F32),
            pltpu.VMEM((chunks, sky_tiles, ROWS, LANES), F32),
            pltpu.VMEM((chunks, sky_tiles, ROWS, LANES), F32),
            pltpu.VMEM((chunks, sky_tiles, ROWS, LANES), F32),
            pltpu.VMEM((pairs, nx - 1, sky_tiles // nx, ROWS, LANES), F32),
            pltpu.VMEM((pairs, ny - 1, sky_tiles // ny, ROWS, LANES), F32),
            pltpu.VMEM((pairs, ny - 1, own, ROWS, LANES), F32),
            pltpu.VMEM((pairs, nx - 1, own, ROWS, LANES), F32),
            pltpu.VMEM((chunks, own // 2, ROWS, LANES), F32),
            pltpu.VMEM((2, TILE_BLOCKS * BLOCK, own_cols), F32),
            dma((2, points * blocks)),
            dma((2,)),
            dma((2, chunks)),
            dma((2, chunks, most)),
            dma((2, chunks, most)),
            dma((2, chunks)),
            dma((2, chunks)),
        ],
        compiler_params=pltpu.CompilerParams(
            collective_id=0, has_side_effects=True, vmem_limit_bytes=67043328
        ),
        name="combine",
    )(images, beams, row_block, col_block, band, row_frac, col_frac)
    numer = summed[0]
    weight = summed[1]
    normalised = numer / jnp.maximum(weight, 0.05)
    return (numer, weight, normalised)


def solution(mesh):
    ny, nx = chip_grid(mesh.shape["pgroup"])
    return jax.shard_map(
        functools.partial(body, ny, nx, mesh.shape["tile"]),
        mesh=mesh,
        in_specs=(
            P(("pgroup", "tile"), None, None),
            P(("pgroup", "tile"), None, None),
            P(("pgroup", "tile")),
            P(("pgroup", "tile")),
            P(("pgroup", "tile"), None),
            P(("pgroup", "tile")),
            P(("pgroup", "tile")),
        ),
        out_specs=(P("tile", "pgroup"), P("tile", "pgroup"), P("tile", "pgroup")),
        check_vma=False,
    )
```

profile of v0, /device:TPU:0, one launch (start us, length us, event | category | flops | bytes accessed | tf_op | source)
XLA Modules:
  0.0 86.5 jit_solution(142165005643393953)
XLA Ops:
  0.6 82.5 %combine.1 = f32[2,512,512]{2,1,0:T(8,128)} custom-call(f32[2,256,2048]{2,1,0:T(8,128)} %images.1, f32[2,256,2048]{2,1,0:T(8,128)} %beams.1, s32[2]{0:T(128)} %row_block.1, s32[2]{0:T(128)} %col_block.1, s32[2,2]{1,0:T(2,128)} %band.1, f32[2]{0:T(128)} %row_frac.1, f32[2]{0:T(128)} %col_frac.1), custom_call_target="tpu_custom_call" | custom-call | tf_op jit(solution)/shard_map/combine/pallas_call | solution.py:393
  83.1 3.4 %maximum_divide_fusion = (f32[512,512]{1,0:T(8,128)}, f32[512,512]{1,0:T(8,128)}, f32[512,512]{1,0:T(8,128)}) fusion(f32[2,512,512]{2,1,0:T(8,128)} %combine.1), kind=kLoop, calls=%fused_computation | loop fusion | flops 524288 | bytes 5242880 | tf_op jit(solution)/shard_map/div | solution.py:428
where the time goes:
time: 86.7 us; the launch traced here: 86.5 us
  Pallas kernels  82.5 us (95%)
  other arithmetic  3.39 us (4%)
    pallas_call x1, Pallas kernels, body(): pl.pallas_call(functools.partial(kernel, ny, nx, n_tile), out_shape=jax.S...  82.5 us
    div x1, other arithmetic, body(): normalised = numer / jnp.maximum(weight, 0.05)  3.39 us

commit v1 on v0

v1 whole, which is shorter than its diff:
```python
import functools
import math

import jax
import jax.numpy as jnp
from jax import lax
from jax.experimental import pallas as pl
from jax.experimental.pallas import tpu as pltpu
from jax.sharding import PartitionSpec as P

TILE_BLOCKS = 4
SKY_COLS = 4096
LANES = 128
BLOCK = 128
PAD = 8
STEP = 64
START = 32
READY = START + PAD
EARLY = ((START, START), (START + STEP, STEP), (BLOCK, START))
MESH = pl.DeviceIdType.MESH
F32 = jnp.float32


def chip_grid(groups):
    chips = groups // 2
    along_x = math.isqrt(chips)
    while chips % along_x:
        along_x -= 1
    return chips // along_x, along_x


def kernel(
    ny, nx, n_tile,
    images, beams, row_block, col_block, band, row_frac, col_frac,
    numer, weight, normalised,
    raw, shaped, halo_out, halo_in, give, take, canvas,
    first_a, first_b, second_a, second_b,
    load_sem, halo_sem, swap_sem, first_sem, second_sem,
):
    points, img_rows, width = images.shape
    blocks = img_rows // BLOCK
    col_tiles = width // LANES
    sky_tiles = SKY_COLS // LANES
    sky_rows = TILE_BLOCKS * BLOCK
    own = sky_tiles // (ny * nx)
    half = own // 2
    per_core = sky_tiles // 2
    empty = 2 * points * blocks * col_tiles
    chunks = len(EARLY) + (TILE_BLOCKS - 1) * (BLOCK // STEP)

    me = lax.axis_index("pgroup")
    tile = lax.axis_index("tile")
    core = lax.rem(me, 2)
    chip = me // 2
    x = lax.rem(chip, nx)
    y = chip // nx
    partner = me + 1 - 2 * core
    x_peers = [(y * nx + lax.rem(x + d, nx)) * 2 + core for d in range(1, nx)]
    y_peers = [(lax.rem(y + d, ny) * nx + x) * 2 + core for d in range(1, ny)]
    counts = (nx, ny)
    places = (x, y)
    peers = (x_peers, y_peers)
    firsts = (first_a, first_b)
    seconds = (second_a, second_b)
    after = lax.rem(tile + 1, n_tile)
    before = lax.rem(tile + n_tile - 1, n_tile)

    pieces = [(img_rows - READY, READY), (img_rows - BLOCK, BLOCK - READY)]
    pieces += [(b * BLOCK, BLOCK) for b in reversed(range(blocks - 1))]
    loads = []
    for k, (low, size) in enumerate(pieces):
        for p in range(points):
            for which, source in enumerate((images, beams)):
                rows = pl.ds(low, size)
                copy = pltpu.make_async_copy(
                    source.at[p, rows], raw.at[which, p, rows], load_sem.at[which, p, k]
                )
                copy.start()
                loads.append((k, copy))

    barrier = pltpu.get_barrier_semaphore()
    near = [{"pgroup": q} for q in [partner] + x_peers + y_peers]
    near += [{"tile": after}, {"tile": before}]
    for device in near:
        pl.semaphore_signal(barrier, inc=1, device_id=device, device_id_type=MESH)

    def clear(index, _):
        shaped[index, :PAD] = jnp.zeros((PAD, LANES), F32)
        shaped[index, PAD + BLOCK :] = jnp.zeros((PAD, LANES), F32)
        return 0

    lax.fori_loop(0, empty, clear, 0, unroll=8)
    shaped[empty] = jnp.zeros((BLOCK + 2 * PAD, LANES), F32)

    first_lane = lax.broadcasted_iota(jnp.int32, (8, LANES), 1) == 0
    across = [(1.0 - col_frac[p], col_frac[p]) for p in range(points)]
    down = [(1.0 - row_frac[p], row_frac[p]) for p in range(points)]
    base_block = [row_block[p] - tile * TILE_BLOCKS for p in range(points)]
    base_tile = [col_block[p] for p in range(points)]

    def loaded(k):
        for at, copy in loads:
            if at == k:
                copy.wait()

    def interpolate(b, low, high):
        def one(r, _):
            source = pl.ds(pl.multiple_of(b * BLOCK + 8 * r, 8), 8)
            target = pl.ds(pl.multiple_of(PAD + 8 * r, 8), 8)
            for p in range(points):
                stay, go = across[p]
                prior = [jnp.zeros((8, LANES), F32)] * 2
                for t in range(col_tiles):
                    lanes = slice(t * LANES, (t + 1) * LANES)
                    beam = raw[1, p, source, lanes]
                    image = raw[0, p, source, lanes]
                    for a, here in enumerate((beam * image, beam * beam)):
                        turned = pltpu.roll(here, 1, 1)
                        moved = jnp.where(first_lane, prior[a], turned)
                        index = ((a * points + p) * blocks + b) * col_tiles + t
                        shaped[index, target] = stay * here + go * moved
                        prior[a] = turned
            return 0

        lax.fori_loop(low // 8, high // 8, one, 0)

    def sum_rows(a, sky_block, sky_tile, start, size):
        total = None
        for p in range(points):
            b = sky_block - base_block[p]
            t = sky_tile - base_tile[p]
            inside = (b >= 0) & (b < blocks) & (t >= 0) & (t < col_tiles)
            index = ((a * points + p) * blocks + b) * col_tiles + t
            index = jnp.where(inside, index, empty)
            shift = band[p, jnp.clip(b, 0, blocks - 1)]
            low = shaped[index, pl.ds(PAD + start - shift, size)]
            high = shaped[index, pl.ds(PAD - 1 + start - shift, size)]
            term = down[p][0] * low + down[p][1] * high
            total = term if total is None else total + term
        return total

    def sky_tile_of(a, which, slot):
        group = slot // half
        count = (ny, nx)[a]
        major, minor = group // count, lax.rem(group, count)
        at = minor * nx + major if a == 0 else major * nx + minor
        return at * own + which * half + lax.rem(slot, half)

    def block_of(a, d):
        size = per_core // counts[a]
        at = places[a] if d == 0 else lax.rem(places[a] + d, counts[a])
        return at * size, size

    def order():
        return [(a, d) for d in range(1, max(nx, ny)) for a in range(2) if d < counts[a]] + [(0, 0), (1, 0)]

    def chunk(m):
        if isinstance(m, int) and m < len(EARLY):
            below, size = EARLY[m]
            return pl.ds(sky_rows - below, size)
        start = sky_rows - BLOCK - STEP * (m - len(EARLY) + 1)
        return pl.ds(pl.multiple_of(start, STEP), STEP)

    def swap(m, a, d):
        first, size = block_of(a, d)
        view = (a, pl.ds(first, size), chunk(m))
        return pltpu.make_async_remote_copy(
            give.at[view], take.at[view], swap_sem.at[0, m, a, d], swap_sem.at[1, m, a, d],
            device_id={"pgroup": partner}, device_id_type=MESH,
        )

    def first_copy(m, a, d):
        first, size = block_of(a, d)
        rows = chunk(m)
        return pltpu.make_async_remote_copy(
            canvas.at[a, pl.ds(first, size), rows], firsts[a].at[d - 1, :, rows],
            first_sem.at[0, m, a, d - 1], first_sem.at[1, m, a, d - 1],
            device_id={"pgroup": peers[a][d - 1]}, device_id_type=MESH,
        )

    def second_copy(m, a, d):
        other = 1 - a
        first, _ = block_of(a, 0)
        at = lax.rem(places[other] + d, counts[other])
        rows = chunk(m)
        return pltpu.make_async_remote_copy(
            canvas.at[a, pl.ds(first + at * half, half), rows], seconds[a].at[d - 1, :, rows],
            second_sem.at[0, m, a, d - 1], second_sem.at[1, m, a, d - 1],
            device_id={"pgroup": peers[other][d - 1]}, device_id_type=MESH,
        )

    use = jnp.where(tile > 0, 1.0, 0.0)

    def put(target, a, which, slot, rows, sky_block, start, size, last, extra):
        sky_tile = sky_tile_of(a, which, slot)
        total = sum_rows(a, sky_block, sky_tile, start, size)
        if extra is not None:
            total = total + extra[a, slot, rows]
        target[a, slot, rows] = total
        if start == 0:
            top = total[:8] + sum_rows(a, sky_block - 1, sky_tile, BLOCK, 8)
            if last:
                top = top + use * halo_in[a, sky_tile]
            target[a, slot, pl.ds(rows.start, 8)] = top

    def build(m, sky_block, start, last=False):
        rows = chunk(m)
        for a, d in order():
            first, count = block_of(a, d)

            def one(s, _):
                put(give, a, 1 - core, first + s, rows, sky_block, start, rows.size, last, None)
                return 0

            lax.fori_loop(0, count, one, 0, unroll=2)
            swap(m, a, d).start()

    def combine(m, sky_block, start, last=False):
        rows = chunk(m)
        for a, d in order():
            first, count = block_of(a, d)
            swap(m, a, d).wait_recv()

            def one(s, _):
                put(canvas, a, core, first + s, rows, sky_block, start, rows.size, last, take)
                return 0

            lax.fori_loop(0, count, one, 0, unroll=2)
            if d:
                first_copy(m, a, d).start()

    halo = pltpu.make_async_remote_copy(
        halo_out, halo_in, halo_sem.at[0], halo_sem.at[1],
        device_id={"tile": after}, device_id_type=MESH,
    )

    def border(sky_tile, _):
        for a in range(2):
            halo_out[a, sky_tile] = sum_rows(a, TILE_BLOCKS - 1, sky_tile, BLOCK, 8)
        return 0

    top = TILE_BLOCKS - 1
    loaded(0)
    interpolate(blocks - 1, BLOCK - READY, BLOCK)
    pl.semaphore_wait(barrier, len(near))
    build(0, top, BLOCK - START)
    loaded(1)
    interpolate(blocks - 1, 0, BLOCK - READY)
    combine(0, top, BLOCK - START)
    build(1, top, START)
    for k, b in enumerate(reversed(range(blocks - 1))):
        loaded(2 + k)
        interpolate(b, 0, BLOCK)
    combine(1, top, START)
    build(2, top, 0)
    lax.fori_loop(0, sky_tiles, border, 0)
    halo.start()
    build(3, top - 1, STEP)
    combine(2, top, 0)

    def spread(i, _):
        at = top - 1 - i
        build(4 + 2 * i, at, 0)
        combine(3 + 2 * i, at, STEP)
        build(5 + 2 * i, at - 1, STEP)
        combine(4 + 2 * i, at, 0)
        return 0

    lax.fori_loop(0, top - 1, spread, 0)
    halo.wait_recv()
    build(chunks - 1, 0, 0, last=True)
    combine(chunks - 2, 0, STEP)
    combine(chunks - 1, 0, 0, last=True)

    def every(step):
        for m in range(len(EARLY)):
            step(m)

        def one(m, _):
            step(m)
            return 0

        lax.fori_loop(len(EARLY), chunks, one, 0)

    def middle(m):
        rows = chunk(m)
        for a in range(2):
            for d in range(1, counts[a]):
                first_copy(m, a, d).wait_recv()
            first, _ = block_of(a, 0)
            for e in range(1, counts[1 - a]):
                at = lax.rem(places[1 - a] + e, counts[1 - a]) * half

                def one(q, _):
                    total = canvas[a, first + at + q, rows]
                    for d in range(counts[a] - 1):
                        total = total + firsts[a][d, at + q, rows]
                    canvas[a, first + at + q, rows] = total
                    return 0

                lax.fori_loop(0, half, one, 0, unroll=True)
                second_copy(m, a, e).start()

    every(middle)

    def finish(m):
        rows = chunk(m)
        for a in range(2):
            for e in range(1, counts[1 - a]):
                second_copy(m, a, e).wait_recv()
        for q in range(half):
            sums = []
            for a in range(2):
                first, _ = block_of(a, 0)
                at = places[1 - a] * half + q
                total = canvas[a, first + at, rows]
                for d in range(counts[a] - 1):
                    total = total + firsts[a][d, at, rows]
                for e in range(counts[1 - a] - 1):
                    total = total + seconds[a][e, q, rows]
                sums.append(total)
            lanes = slice(q * LANES, (q + 1) * LANES)
            numer[rows, lanes] = sums[0]
            weight[rows, lanes] = sums[1]
            normalised[rows, lanes] = sums[0] / jnp.maximum(sums[1], 0.05)

    every(finish)

    def drain(m):
        for a in range(2):
            for d in range(counts[a]):
                swap(m, a, d).wait_send()
                if d:
                    first_copy(m, a, d).wait_send()
            for e in range(1, counts[1 - a]):
                second_copy(m, a, e).wait_send()

    every(drain)
    halo.wait_send()


def body(ny, nx, n_tile, images, beams, row_block, col_block, band, row_frac, col_frac):
    points, img_rows, width = images.shape
    blocks = img_rows // BLOCK
    col_tiles = width // LANES
    sky_tiles = SKY_COLS // LANES
    sky_rows = TILE_BLOCKS * BLOCK
    half = sky_tiles // (2 * ny * nx)
    per_core = sky_tiles // 2
    chunks = len(EARLY) + (TILE_BLOCKS - 1) * (BLOCK // STEP)
    own_cols = half * LANES
    most = max(nx, ny)
    dma = pltpu.SemaphoreType.DMA
    smem = pl.BlockSpec(memory_space=pltpu.SMEM)
    vmem = pl.BlockSpec(memory_space=pltpu.VMEM)
    out = pltpu.VMEM((sky_rows, own_cols), F32)
    numer, weight, normalised = pl.pallas_call(
        functools.partial(kernel, ny, nx, n_tile),
        out_shape=(out, out, out),
        in_specs=[pl.BlockSpec(memory_space=pl.ANY)] * 2 + [smem] * 5,
        out_specs=(vmem, vmem, vmem),
        scratch_shapes=[
            pltpu.VMEM((2, points, img_rows, width), F32),
            pltpu.VMEM((2 * points * blocks * col_tiles + 1, BLOCK + 2 * PAD, LANES), F32),
            pltpu.VMEM((2, sky_tiles, 8, LANES), F32),
            pltpu.VMEM((2, sky_tiles, 8, LANES), F32),
            pltpu.VMEM((2, per_core, sky_rows, LANES), F32),
            pltpu.VMEM((2, per_core, sky_rows, LANES), F32),
            pltpu.VMEM((2, per_core, sky_rows, LANES), F32),
            pltpu.VMEM((nx - 1, ny * half, sky_rows, LANES), F32),
            pltpu.VMEM((ny - 1, nx * half, sky_rows, LANES), F32),
            pltpu.VMEM((ny - 1, half, sky_rows, LANES), F32),
            pltpu.VMEM((nx - 1, half, sky_rows, LANES), F32),
            dma((2, points, blocks + 1)),
            dma((2,)),
            dma((2, chunks, 2, most)),
            dma((2, chunks, 2, most - 1)),
            dma((2, chunks, 2, most - 1)),
        ],
        compiler_params=pltpu.CompilerParams(
            collective_id=0, has_side_effects=True, vmem_limit_bytes=56 * 1024 * 1024
        ),
        name="combine",
    )(images, beams, row_block, col_block, band, row_frac, col_frac)
    return (numer, weight, normalised)


def solution(mesh):
    ny, nx = chip_grid(mesh.shape["pgroup"])
    return jax.shard_map(
        functools.partial(body, ny, nx, mesh.shape["tile"]),
        mesh=mesh,
        in_specs=(
            P(("pgroup", "tile"), None, None),
            P(("pgroup", "tile"), None, None),
            P(("pgroup", "tile")),
            P(("pgroup", "tile")),
            P(("pgroup", "tile"), None),
            P(("pgroup", "tile")),
            P(("pgroup", "tile")),
        ),
        out_specs=(P("tile", "pgroup"), P("tile", "pgroup"), P("tile", "pgroup")),
        check_vma=False,
    )
```

time: 86.7 us -> 84.6 us (0.976)
  other arithmetic: 3.39 us -> 0 us
  local copies, waits for them, and re-layouts: 0 us -> 2.91 us
  Pallas kernels: 82.5 us -> 80.9 us
    div x1 -> x0, other arithmetic: 3.39 us -> none  [body(): normalised = numer / jnp.maximum(weight, 0.05)]
    unnamed x0 -> x3, local copies, waits for them, and re-layouts: none -> 2.91 us
    pallas_call x1, Pallas kernels: 82.5 us -> 80.9 us  [body(): pl.pallas_call(functools.partial(kernel, ny, nx, n_tile), out_shape=(out,...]
where the time goes in v1:
time: 84.6 us; the launch traced here: 84.5 us
  Pallas kernels  80.9 us (96%)
  local copies, waits for them, and re-layouts  2.91 us (3%)
    pallas_call x1, Pallas kernels, body(): pl.pallas_call(functools.partial(kernel, ny, nx, n_tile), out_shape=(out,...  80.9 us
    unnamed x3, local copies, waits for them, and re-layouts  2.91 us

profile of v1, /device:TPU:0, one launch (start us, length us, event | category | flops | bytes accessed | tf_op | source)
XLA Modules:
  0.0 84.5 jit_solution(18107235159459876173)
XLA Ops:
  0.6 80.9 %combine.1 = (f32[512,512]{1,0:T(8,128)S(1)}, f32[512,512]{1,0:T(8,128)S(1)}, f32[512,512]{1,0:T(8,128)S(1)}) custom-call(f32[2,256,2048]{2,1,0:T(8,128)} %images.1, f32[2,256,2048]{2,1,0:T(8,128)} %beams.1, s32[2]{0:T(128)} %row_block.1, s32[2]{0:T(128)} %col_block.1, s32[2,2]{1,0:T(2,128)} %band.1, f32[2]{0:T(128)} %row_frac.1, f32[2]{0:T(128)} %col_frac.1), custom_call_target="tpu_custom_call" | custom-call | tf_op jit(solution)/shard_map/combine/pallas_call | solution.py:357
  81.6 1.0 %copy.13 = f32[512,512]{1,0:T(8,128)} copy(f32[512,512]{1,0:T(8,128)S(1)} %get-tuple-element.3) | data formatting | bytes 2097152
  82.5 1.0 %copy.14 = f32[512,512]{1,0:T(8,128)} copy(f32[512,512]{1,0:T(8,128)S(1)} %get-tuple-element.4) | data formatting | bytes 2097152
  83.5 1.0 %copy.15 = f32[512,512]{1,0:T(8,128)} copy(f32[512,512]{1,0:T(8,128)S(1)} %get-tuple-element.5) | data formatting | bytes 2097152

commit v2 on v1

v2 whole, which is shorter than its diff:
```python
import functools
import math

import jax
import jax.numpy as jnp
from jax import lax
from jax.experimental import pallas as pl
from jax.experimental.pallas import tpu as pltpu
from jax.sharding import PartitionSpec as P

TILE_BLOCKS = 4
SKY_COLS = 4096
LANES = 128
BLOCK = 128
PAD = 8
STEP = 64
START = 32
READY = START + PAD
FINE = 2
EARLY = ((START, START), (START + STEP, STEP), (BLOCK, START))
MESH = pl.DeviceIdType.MESH
F32 = jnp.float32


def chip_grid(groups):
    chips = groups // 2
    along_x = math.isqrt(chips)
    while chips % along_x:
        along_x -= 1
    return chips // along_x, along_x


def kernel(
    ny, nx, n_tile,
    images, beams, row_block_in, col_block_in, band_in, row_frac_in, col_frac_in,
    numer, weight, normalised,
    row_block, col_block, band, row_frac, col_frac,
    raw, shaped, halo_out, halo_in, give, take, canvas,
    first_a, first_b, second,
    small_sem, load_sem, halo_sem, entered, swap_sem, first_sem, second_sem, send_sem,
):
    points, img_rows, width = images.shape
    blocks = img_rows // BLOCK
    col_tiles = width // LANES
    sky_tiles = SKY_COLS // LANES
    sky_rows = TILE_BLOCKS * BLOCK
    own = sky_tiles // (ny * nx)
    half = own // 2
    per_core = sky_tiles // 2
    empty = points * blocks * col_tiles
    chunks = len(EARLY) + (TILE_BLOCKS - 1) * (BLOCK // STEP)

    me = lax.axis_index("pgroup")
    tile = lax.axis_index("tile")
    core = lax.rem(me, 2)
    chip = me // 2
    x = lax.rem(chip, nx)
    y = chip // nx
    partner = me + 1 - 2 * core
    x_peers = [(y * nx + lax.rem(x + d, nx)) * 2 + core for d in range(1, nx)]
    y_peers = [(lax.rem(y + d, ny) * nx + x) * 2 + core for d in range(1, ny)]
    counts = (nx, ny)
    most = max(nx, ny)
    places = (x, y)
    peers = (x_peers, y_peers)
    firsts = (first_a, first_b)
    seconds = (second.at[pl.ds(0, ny - 1)], second.at[pl.ds(ny - 1, nx - 1)])
    after = lax.rem(tile + 1, n_tile)
    before = lax.rem(tile + n_tile - 1, n_tile)

    pieces = [(img_rows - READY, READY), (img_rows - BLOCK, BLOCK - READY)]
    pieces += [(b * BLOCK, BLOCK) for b in reversed(range(blocks - 1))]
    for k, (low, size) in enumerate(pieces):
        for p in range(points):
            for which, source in enumerate((images, beams)):
                rows = pl.ds(low, size)
                pltpu.make_async_copy(
                    source.at[p, rows], raw.at[which, p, rows], load_sem.at[k]
                ).start()
        if k == 0:
            small = [
                pltpu.make_async_copy(source, target, small_sem.at[n])
                for n, (source, target) in enumerate((
                    (row_block_in, row_block), (col_block_in, col_block), (band_in, band),
                    (row_frac_in, row_frac), (col_frac_in, col_frac),
                ))
            ]
            for copy in small:
                copy.start()

    barrier = pltpu.get_barrier_semaphore()
    near = [partner] + x_peers + y_peers
    for q in near:
        pl.semaphore_signal(barrier, inc=1, device_id={"pgroup": q}, device_id_type=MESH)

    @pl.when(tile < n_tile - 1)
    def _():
        pl.semaphore_signal(barrier, inc=1, device_id={"tile": after}, device_id_type=MESH)

    def clear(index, _):
        for a in range(2):
            shaped[a, index, :PAD] = jnp.zeros((PAD, LANES), F32)
            shaped[a, index, PAD + BLOCK :] = jnp.zeros((PAD, LANES), F32)
        return 0

    lax.fori_loop(0, empty, clear, 0, unroll=8)
    for a in range(2):
        shaped[a, empty] = jnp.zeros((BLOCK + 2 * PAD, LANES), F32)
    for copy in small:
        copy.wait()

    first_lane = lax.broadcasted_iota(jnp.int32, (8, LANES), 1) == 0
    across = [(1.0 - col_frac[p], col_frac[p]) for p in range(points)]
    down = [(1.0 - row_frac[p], row_frac[p]) for p in range(points)]
    base_block = [row_block[p] - tile * TILE_BLOCKS for p in range(points)]
    base_tile = [col_block[p] for p in range(points)]

    def loaded(k):
        low, size = pieces[k]
        view = raw.at[:, :, pl.ds(low, size)]
        pltpu.make_async_copy(view, view, load_sem.at[k]).wait()

    def interpolate(b, low, high):
        def one(r, _):
            source = pl.ds(pl.multiple_of(b * BLOCK + 8 * r, 8), 8)
            target = pl.ds(pl.multiple_of(PAD + 8 * r, 8), 8)
            for p in range(points):
                stay, go = across[p]
                prior = [jnp.zeros((8, LANES), F32)] * 2
                for t in range(col_tiles):
                    lanes = slice(t * LANES, (t + 1) * LANES)
                    beam = raw[1, p, source, lanes]
                    image = raw[0, p, source, lanes]
                    for a, here in enumerate((beam * image, beam * beam)):
                        turned = pltpu.roll(here, 1, 1)
                        moved = jnp.where(first_lane, prior[a], turned)
                        shaped[a, (p * blocks + b) * col_tiles + t, target] = stay * here + go * moved
                        prior[a] = turned
            return 0

        lax.fori_loop(low // 8, high // 8, one, 0)

    def block_terms(sky_block):
        terms = []
        for p in range(points):
            b = sky_block - base_block[p]
            within = (b >= 0) & (b < blocks)
            b = jnp.clip(b, 0, blocks - 1)
            shift = band[p, b]
            at = jnp.where(within, base_tile[p], sky_tiles)
            terms.append((at, (p * blocks + b) * col_tiles - base_tile[p], PAD - shift))
        return terms

    def indices(terms, sky_tile):
        found = []
        for at, base, _ in terms:
            t = sky_tile - at
            found.append(jnp.where((t >= 0) & (t < col_tiles), base + sky_tile, empty))
        return found

    def sum_rows(a, terms, index, start, size):
        total = None
        for p in range(points):
            at = terms[p][2] + start
            low = shaped[a, index[p], pl.ds(at, size)]
            high = shaped[a, index[p], pl.ds(at - 1, size)]
            term = down[p][0] * low + down[p][1] * high
            total = term if total is None else total + term
        return total

    def slot_of(a, chip_at):
        if a == 1:
            return chip_at * half
        return (lax.rem(chip_at, nx) * ny + chip_at // nx) * half

    def block_of(a, d):
        size = per_core // counts[a]
        at = places[a] if d == 0 else lax.rem(places[a] + d, counts[a])
        return at * size, size

    def order():
        return [(a, d) for d in range(1, max(nx, ny)) for a in range(2) if d < counts[a]] + [(0, 0), (1, 0)]

    def chunk(m):
        if isinstance(m, int) and m < len(EARLY):
            below, size = EARLY[m]
            return pl.ds(sky_rows - below, size)
        start = sky_rows - BLOCK - STEP * (m - len(EARLY) + 1)
        return pl.ds(pl.multiple_of(start, STEP), STEP)

    def swap(m, a=None, d=None):
        if a is None:
            view = (slice(None), slice(None), chunk(m))
            sem = swap_sem.at[m + FINE * (2 * most - 1)]
        else:
            first, size = block_of(a, d)
            view = (a, pl.ds(first, size), chunk(m))
            sem = swap_sem.at[(m * 2 + a) * most + d]
        return pltpu.make_async_remote_copy(
            give.at[view], take.at[view], send_sem.at[0], sem,
            device_id={"pgroup": partner}, device_id_type=MESH,
        )

    def first_copy(m, a, d):
        first, size = block_of(a, d)
        rows = chunk(m)
        return pltpu.make_async_remote_copy(
            canvas.at[a, pl.ds(first, size), rows], firsts[a].at[d - 1, :, rows],
            send_sem.at[1 + a], first_sem.at[m, a],
            device_id={"pgroup": peers[a][d - 1]}, device_id_type=MESH,
        )

    def second_copy(m, a, d):
        other = 1 - a
        first, _ = block_of(a, 0)
        at = lax.rem(places[other] + d, counts[other])
        rows = chunk(m)
        return pltpu.make_async_remote_copy(
            canvas.at[a, pl.ds(first + at * half, half), rows], seconds[a].at[d - 1, :, rows],
            send_sem.at[3 + a], second_sem.at[m],
            device_id={"pgroup": peers[other][d - 1]}, device_id_type=MESH,
        )

    def arrived(view, sem):
        pltpu.make_async_copy(view, view, sem).wait()

    def put(target, a, slot, sky_tile, rows, start, terms, index, above, index_above, last, extra):
        total = sum_rows(a, terms, index, start, rows.size)
        if extra is not None:
            total = total + extra[a, slot, rows]
        target[a, slot, rows] = total
        if start == 0:
            top = total[:8] + sum_rows(a, above, index_above, BLOCK, 8)
            if last:
                top = top + halo_in[a, sky_tile]
            target[a, slot, pl.ds(rows.start, 8)] = top

    def cover(target, which, m, sky_block, start, arrays, chips, last, extra):
        rows = chunk(m)
        terms = block_terms(sky_block)
        above = block_terms(sky_block - 1) if start == 0 else None

        def one(n, _):
            chip_at = chips(n)
            for q in range(half):
                sky_tile = chip_at * own + which * half + q
                index = indices(terms, sky_tile)
                index_above = indices(above, sky_tile) if start == 0 else None
                for a in arrays:
                    put(
                        target, a, slot_of(a, chip_at) + q, sky_tile, rows, start,
                        terms, index, above, index_above, last, extra,
                    )
            return 0

        return one

    def part(target, which, m, sky_block, start, a, d, extra):
        at = places[a] if d == 0 else lax.rem(places[a] + d, counts[a])
        chips = (lambda n: n * nx + at) if a == 0 else (lambda n: at * nx + n)
        one = cover(target, which, m, sky_block, start, (a,), chips, False, extra)
        lax.fori_loop(0, counts[1 - a], one, 0)

    def build(m, sky_block, start, last=False):
        if isinstance(m, int) and m < FINE:
            for a, d in order():
                part(give, 1 - core, m, sky_block, start, a, d, None)
            return
        one = cover(give, 1 - core, m, sky_block, start, (0, 1), lambda n: n, last, None)
        lax.fori_loop(0, ny * nx, one, 0)
        swap(m).start()

    def offer(m):
        for a, d in order():
            swap(m, a, d).start()

    def combine(m, sky_block, start, last=False):
        if isinstance(m, int) and m < FINE:
            for a, d in order():
                swap(m, a, d).wait_recv()
                part(canvas, core, m, sky_block, start, a, d, take)
                if d:
                    first_copy(m, a, d).start()
            return
        swap(m).wait_recv()
        one = cover(canvas, core, m, sky_block, start, (0, 1), lambda n: n, last, take)
        lax.fori_loop(0, ny * nx, one, 0)
        for a, d in order():
            if d:
                first_copy(m, a, d).start()

    halo = pltpu.make_async_remote_copy(
        halo_out, halo_in, halo_sem.at[0], halo_sem.at[1],
        device_id={"tile": after}, device_id_type=MESH,
    )

    top = TILE_BLOCKS - 1
    top_terms = block_terms(top)

    def border(sky_tile, _):
        index = indices(top_terms, sky_tile)
        for a in range(2):
            halo_out[a, sky_tile] = sum_rows(a, top_terms, index, BLOCK, 8)
        return 0

    loaded(0)
    interpolate(blocks - 1, BLOCK - READY, BLOCK)
    build(0, top, BLOCK - START)
    pl.semaphore_wait(barrier, len(near) + jnp.where(tile > 0, 1, 0))
    offer(0)
    loaded(1)
    interpolate(blocks - 1, 0, BLOCK - READY)

    @pl.when(tile > 0)
    def _():
        pl.semaphore_signal(entered, inc=1, device_id={"tile": before}, device_id_type=MESH)

    @pl.when(tile == 0)
    def _():
        halo_in[...] = jnp.zeros(halo_in.shape, F32)

    combine(0, top, BLOCK - START)
    build(1, top, START)
    offer(1)
    for k, b in enumerate(reversed(range(blocks - 1))):
        loaded(2 + k)
        interpolate(b, 0, BLOCK)
    combine(1, top, START)
    build(2, top, 0)
    lax.fori_loop(0, sky_tiles, border, 0, unroll=4)

    @pl.when(tile < n_tile - 1)
    def _():
        pl.semaphore_wait(entered, 1)
        halo.start()

    build(3, top - 1, STEP)
    combine(2, top, 0)

    def spread(i, _):
        at = top - 1 - i
        build(4 + 2 * i, at, 0)
        combine(3 + 2 * i, at, STEP)
        build(5 + 2 * i, at - 1, STEP)
        combine(4 + 2 * i, at, 0)
        return 0

    lax.fori_loop(0, top - 1, spread, 0)

    @pl.when(tile > 0)
    def _():
        halo.wait_recv()

    build(chunks - 1, 0, 0, last=True)
    combine(chunks - 2, 0, STEP)
    combine(chunks - 1, 0, 0, last=True)

    def every(step):
        for m in range(len(EARLY)):
            step(m)

        def one(m, _):
            step(m)
            return 0

        lax.fori_loop(len(EARLY), chunks, one, 0)

    def middle(m):
        rows = chunk(m)
        for a in range(2):
            arrived(firsts[a].at[:, :, rows], first_sem.at[m, a])
            first, _ = block_of(a, 0)
            for e in range(1, counts[1 - a]):
                at = lax.rem(places[1 - a] + e, counts[1 - a]) * half

                def one(q, _):
                    total = canvas[a, first + at + q, rows]
                    for d in range(counts[a] - 1):
                        total = total + firsts[a][d, at + q, rows]
                    canvas[a, first + at + q, rows] = total
                    return 0

                lax.fori_loop(0, half, one, 0, unroll=True)
                second_copy(m, a, e).start()

    every(middle)

    def finish(m):
        rows = chunk(m)
        arrived(second.at[:, :, rows], second_sem.at[m])
        for q in range(half):
            sums = []
            for a in range(2):
                first, _ = block_of(a, 0)
                at = places[1 - a] * half + q
                total = canvas[a, first + at, rows]
                for d in range(counts[a] - 1):
                    total = total + firsts[a][d, at, rows]
                for e in range(counts[1 - a] - 1):
                    total = total + seconds[a][e, q, rows]
                sums.append(total)
            lanes = slice(q * LANES, (q + 1) * LANES)
            numer[rows, lanes] = sums[0]
            weight[rows, lanes] = sums[1]
            normalised[rows, lanes] = sums[0] / jnp.maximum(sums[1], 0.05)

    every(finish)

    arrived(give, send_sem.at[0])
    for a in range(2):
        arrived(firsts[a], send_sem.at[1 + a])
        arrived(seconds[a], send_sem.at[3 + a])

    @pl.when(tile < n_tile - 1)
    def _():
        halo.wait_send()


def copy_out(numer, weight, normalised, numer_out, weight_out, normalised_out, sem):
    pairs = ((numer, numer_out), (weight, weight_out), (normalised, normalised_out))
    copies = [pltpu.make_async_copy(a, b, sem.at[n]) for n, (a, b) in enumerate(pairs)]
    for copy in copies:
        copy.start()
    for copy in copies:
        copy.wait()


def body(ny, nx, n_tile, images, beams, row_block, col_block, band, row_frac, col_frac):
    points, img_rows, width = images.shape
    blocks = img_rows // BLOCK
    col_tiles = width // LANES
    sky_tiles = SKY_COLS // LANES
    sky_rows = TILE_BLOCKS * BLOCK
    half = sky_tiles // (2 * ny * nx)
    per_core = sky_tiles // 2
    chunks = len(EARLY) + (TILE_BLOCKS - 1) * (BLOCK // STEP)
    own_cols = half * LANES
    most = max(nx, ny)
    dma = pltpu.SemaphoreType.DMA
    anywhere = pl.BlockSpec(memory_space=pl.ANY)
    scalars = [pltpu.SMEM(v.shape, v.dtype) for v in (row_block, col_block, band, row_frac, col_frac)]
    vmem = pl.BlockSpec(memory_space=pltpu.VMEM)
    out = pltpu.VMEM((sky_rows, own_cols), F32)
    numer, weight, normalised = pl.pallas_call(
        functools.partial(kernel, ny, nx, n_tile),
        out_shape=(out, out, out),
        in_specs=[anywhere] * 7,
        out_specs=(vmem, vmem, vmem),
        scratch_shapes=scalars + [
            pltpu.VMEM((2, points, img_rows, width), F32),
            pltpu.VMEM((2, points * blocks * col_tiles + 1, BLOCK + 2 * PAD, LANES), F32),
            pltpu.VMEM((2, sky_tiles, 8, LANES), F32),
            pltpu.VMEM((2, sky_tiles, 8, LANES), F32),
            pltpu.VMEM((2, per_core, sky_rows, LANES), F32),
            pltpu.VMEM((2, per_core, sky_rows, LANES), F32),
            pltpu.VMEM((2, per_core, sky_rows, LANES), F32),
            pltpu.VMEM((nx - 1, ny * half, sky_rows, LANES), F32),
            pltpu.VMEM((ny - 1, nx * half, sky_rows, LANES), F32),
            pltpu.VMEM((ny - 1 + nx - 1, half, sky_rows, LANES), F32),
            dma((5,)),
            dma((blocks + 1,)),
            dma((2,)),
            pltpu.SemaphoreType.REGULAR,
            dma((chunks + FINE * (2 * most - 1),)),
            dma((chunks, 2)),
            dma((chunks,)),
            dma((5,)),
        ],
        compiler_params=pltpu.CompilerParams(
            collective_id=0, has_side_effects=True, vmem_limit_bytes=56 * 1024 * 1024
        ),
        name="combine",
    )(images, beams, row_block, col_block, band, row_frac, col_frac)
    flat = jax.ShapeDtypeStruct((sky_rows, own_cols), F32)
    return pl.pallas_call(
        copy_out,
        out_shape=(flat, flat, flat),
        in_specs=[vmem] * 3,
        out_specs=(anywhere,) * 3,
        scratch_shapes=[dma((3,))],
        name="copy_out",
    )(*[pltpu.with_memory_space_constraint(v, pltpu.VMEM) for v in (numer, weight, normalised)])


def solution(mesh):
    ny, nx = chip_grid(mesh.shape["pgroup"])
    return jax.shard_map(
        functools.partial(body, ny, nx, mesh.shape["tile"]),
        mesh=mesh,
        in_specs=(
            P(("pgroup", "tile"), None, None),
            P(("pgroup", "tile"), None, None),
            P(("pgroup", "tile")),
            P(("pgroup", "tile")),
            P(("pgroup", "tile"), None),
            P(("pgroup", "tile")),
            P(("pgroup", "tile")),
        ),
        out_specs=(P("tile", "pgroup"), P("tile", "pgroup"), P("tile", "pgroup")),
        check_vma=False,
    )
```

time: 84.6 us -> 78.7 us (0.930)
  Pallas kernels: 80.9 us -> 77.9 us
  local copies, waits for them, and re-layouts: 2.91 us -> 0 us
    pallas_call x1, Pallas kernels: 80.9 us -> 76.2 us  [body(): pl.pallas_call(functools.partial(kernel, ny, nx, n_tile), out_shape=(out,...]
    unnamed x3 -> x0, local copies, waits for them, and re-layouts: 2.91 us -> none
    pallas_call x0 -> x1, Pallas kernels: none -> 1.69 us  [body(): pl.pallas_call(copy_out, out_shape=(flat, flat, flat), in_specs=[vmem] *...]
where the time goes in v2:
time: 78.7 us; the launch traced here: 78.5 us
  Pallas kernels  77.9 us (99%)
    pallas_call x1, Pallas kernels, body(): pl.pallas_call(functools.partial(kernel, ny, nx, n_tile), out_shape=(out,...  76.2 us
    pallas_call x1, Pallas kernels, body(): pl.pallas_call(copy_out, out_shape=(flat, flat, flat), in_specs=[vmem] *...  1.69 us

profile of v2, /device:TPU:0, one launch (start us, length us, event | category | flops | bytes accessed | tf_op | source)
XLA Modules:
  0.0 78.5 jit_solution(9250938116533863212)
XLA Ops:
  0.6 76.2 %combine.1 = (f32[512,512]{1,0:T(8,128)S(1)}, f32[512,512]{1,0:T(8,128)S(1)}, f32[512,512]{1,0:T(8,128)S(1)}) custom-call(f32[2,256,2048]{2,1,0:T(8,128)} %images.1, f32[2,256,2048]{2,1,0:T(8,128)} %beams.1, s32[2]{0:T(128)} %row_block_in.1, s32[2]{0:T(128)} %col_block_in.1, s32[2,2]{1,0:T(2,128)} %band_in.1, f32[2]{0:T(128)} %row_frac_in.1, f32[2]{0:T(128)} %col_frac_in.1), custom_call_target="tpu_custom_call" | custom-call | tf_op jit(solution)/shard_map/combine/pallas_call | solution.py:444
  76.8 1.7 %copy_out.1 = (f32[512,512]{1,0:T(8,128)}, f32[512,512]{1,0:T(8,128)}, f32[512,512]{1,0:T(8,128)}) custom-call(f32[512,512]{1,0:T(8,128)S(1)} %get-tuple-element.6.numer, f32[512,512]{1,0:T(8,128)S(1)} %get-tuple-element.7.weight, f32[512,512]{1,0:T(8,128)S(1)} %get-tuple-element.8.normalised), custom_call_target="tpu_custom_call" | custom-call | tf_op jit(solution)/shard_map/copy_out/pallas_call | solution.py:475

commit v3 on v2

--- a/solution.py
+++ b/solution.py
@@ -16,8 +16,9 @@
 STEP = 64
 START = 32
 READY = START + PAD
-FINE = 2
-EARLY = ((START, START), (START + STEP, STEP), (BLOCK, START))
+PIECES = ((104, 128), (88, 104), (0, 88))
+EARLY = ((16, 16), (32, 16), (64, 32), (BLOCK, STEP))
+FINE = len(EARLY)
 MESH = pl.DeviceIdType.MESH
 F32 = jnp.float32
 
@@ -36,7 +37,7 @@
     numer, weight, normalised,
     row_block, col_block, band, row_frac, col_frac,
     raw, shaped, halo_out, halo_in, give, take, canvas,
-    first_a, first_b, second,
+    inbox,
     small_sem, load_sem, halo_sem, entered, swap_sem, first_sem, second_sem, send_sem,
 ):
     points, img_rows, width = images.shape
@@ -63,30 +64,38 @@
     most = max(nx, ny)
     places = (x, y)
     peers = (x_peers, y_peers)
-    firsts = (first_a, first_b)
-    seconds = (second.at[pl.ds(0, ny - 1)], second.at[pl.ds(ny - 1, nx - 1)])
+    sizes = (per_core // nx, per_core // ny)
+    offsets = (0, (nx - 1) * sizes[0])
+    first_tiles = offsets[1] + (ny - 1) * sizes[1]
+    second_tiles = (first_tiles, first_tiles + (ny - 1) * half)
+    every_tile = second_tiles[1] + (nx - 1) * half
     after = lax.rem(tile + 1, n_tile)
     before = lax.rem(tile + n_tile - 1, n_tile)
 
-    pieces = [(img_rows - READY, READY), (img_rows - BLOCK, BLOCK - READY)]
+    pieces = [(img_rows - BLOCK + low, high - low) for low, high in PIECES]
     pieces += [(b * BLOCK, BLOCK) for b in reversed(range(blocks - 1))]
-    for k, (low, size) in enumerate(pieces):
+
+    def load(k):
+        low, size = pieces[k]
         for p in range(points):
             for which, source in enumerate((images, beams)):
                 rows = pl.ds(low, size)
                 pltpu.make_async_copy(
                     source.at[p, rows], raw.at[which, p, rows], load_sem.at[k]
                 ).start()
-        if k == 0:
-            small = [
-                pltpu.make_async_copy(source, target, small_sem.at[n])
-                for n, (source, target) in enumerate((
-                    (row_block_in, row_block), (col_block_in, col_block), (band_in, band),
-                    (row_frac_in, row_frac), (col_frac_in, col_frac),
-                ))
-            ]
-            for copy in small:
-                copy.start()
+
+    load(0)
+    small = [
+        pltpu.make_async_copy(source, target, small_sem.at[n])
+        for n, (source, target) in enumerate((
+            (row_block_in, row_block), (col_block_in, col_block), (band_in, band),
+            (row_frac_in, row_frac), (col_frac_in, col_frac),
+        ))
+    ]
+    for copy in small:
+        copy.start()
+    for k in range(1, len(pieces)):
+        load(k)
 
     barrier = pltpu.get_barrier_semaphore()
     near = [partner] + x_peers + y_peers
@@ -120,7 +129,7 @@
         view = raw.at[:, :, pl.ds(low, size)]
         pltpu.make_async_copy(view, view, load_sem.at[k]).wait()
 
-    def interpolate(b, low, high):
+    def interpolate(b, low, high, unroll):
         def one(r, _):
             source = pl.ds(pl.multiple_of(b * BLOCK + 8 * r, 8), 8)
             target = pl.ds(pl.multiple_of(PAD + 8 * r, 8), 8)
@@ -138,7 +147,7 @@
                         prior[a] = turned
             return 0
 
-        lax.fori_loop(low // 8, high // 8, one, 0)
+        lax.fori_loop(low // 8, high // 8, one, 0, unroll=unroll)
 
     def block_terms(sky_block):
         terms = []
@@ -173,13 +182,13 @@
             return chip_at * half
         return (lax.rem(chip_at, nx) * ny + chip_at // nx) * half
 
+    def place_of(a, d):
+        return places[a] if d == 0 else lax.rem(places[a] + d, counts[a])
+
     def block_of(a, d):
-        size = per_core // counts[a]
-        at = places[a] if d == 0 else lax.rem(places[a] + d, counts[a])
-        return at * size, size
-
-    def order():
-        return [(a, d) for d in range(1, max(nx, ny)) for a in range(2) if d < counts[a]] + [(0, 0), (1, 0)]
+        return pl.ds(place_of(a, d) * sizes[a], sizes[a])
+
+    remote = [(a, d) for d in range(1, most) for a in range(2) if d < counts[a]]
 
     def chunk(m):
         if isinstance(m, int) and m < len(EARLY):
@@ -188,37 +197,40 @@
         start = sky_rows - BLOCK - STEP * (m - len(EARLY) + 1)
         return pl.ds(pl.multiple_of(start, STEP), STEP)
 
-    def swap(m, a=None, d=None):
-        if a is None:
-            view = (slice(None), slice(None), chunk(m))
-            sem = swap_sem.at[m + FINE * (2 * most - 1)]
-        else:
-            first, size = block_of(a, d)
-            view = (a, pl.ds(first, size), chunk(m))
-            sem = swap_sem.at[(m * 2 + a) * most + d]
+    def swap(view, sem):
         return pltpu.make_async_remote_copy(
-            give.at[view], take.at[view], send_sem.at[0], sem,
+            give.at[view], take.at[view], send_sem.at[0], swap_sem.at[sem],
             device_id={"pgroup": partner}, device_id_type=MESH,
         )
 
+    def swap_part(m, n):
+        a, d = remote[n]
+        return swap((a, block_of(a, d), chunk(m)), m * len(remote) + n)
+
+    def swap_home(a):
+        rows = pl.ds(sky_rows - BLOCK, BLOCK)
+        return swap((a, block_of(a, 0), rows), FINE * len(remote) + a)
+
+    def swap_all(m):
+        return swap((slice(None), slice(None), chunk(m)), FINE * len(remote) + 2 + m - FINE)
+
     def first_copy(m, a, d):
-        first, size = block_of(a, d)
         rows = chunk(m)
+        at = pl.ds(offsets[a] + (d - 1) * sizes[a], sizes[a])
         return pltpu.make_async_remote_copy(
-            canvas.at[a, pl.ds(first, size), rows], firsts[a].at[d - 1, :, rows],
-            send_sem.at[1 + a], first_sem.at[m, a],
+            canvas.at[a, block_of(a, d), rows], inbox.at[at, rows],
+            send_sem.at[1], first_sem.at[m],
             device_id={"pgroup": peers[a][d - 1]}, device_id_type=MESH,
         )
 
     def second_copy(m, a, d):
-        other = 1 - a
-        first, _ = block_of(a, 0)
-        at = lax.rem(places[other] + d, counts[other])
         rows = chunk(m)
+        source = place_of(a, 0) * sizes[a] + place_of(1 - a, d) * half
+        at = pl.ds(second_tiles[a] + (d - 1) * half, half)
         return pltpu.make_async_remote_copy(
-            canvas.at[a, pl.ds(first + at * half, half), rows], seconds[a].at[d - 1, :, rows],
-            send_sem.at[3 + a], second_sem.at[m],
-            device_id={"pgroup": peers[other][d - 1]}, device_id_type=MESH,
+            canvas.at[a, pl.ds(source, half), rows], inbox.at[at, rows],
+            send_sem.at[1], second_sem.at[m],
+            device_id={"pgroup": peers[1 - a][d - 1]}, device_id_type=MESH,
         )
 
     def arrived(view, sem):
@@ -235,8 +247,7 @@
                 top = top + halo_in[a, sky_tile]
             target[a, slot, pl.ds(rows.start, 8)] = top
 
-    def cover(target, which, m, sky_block, start, arrays, chips, last, extra):
-        rows = chunk(m)
+    def cover(target, which, rows, sky_block, start, arrays, chips, last, extra):
         terms = block_terms(sky_block)
         above = block_terms(sky_block - 1) if start == 0 else None
 
@@ -255,39 +266,43 @@
 
         return one
 
-    def part(target, which, m, sky_block, start, a, d, extra):
-        at = places[a] if d == 0 else lax.rem(places[a] + d, counts[a])
+    def part(target, which, rows, start, a, d, extra):
+        at = place_of(a, d)
         chips = (lambda n: n * nx + at) if a == 0 else (lambda n: at * nx + n)
-        one = cover(target, which, m, sky_block, start, (a,), chips, False, extra)
+        one = cover(target, which, rows, TILE_BLOCKS - 1, start, (a,), chips, False, extra)
         lax.fori_loop(0, counts[1 - a], one, 0)
 
+    def begin(m):
+        for n, (a, d) in enumerate(remote):
+            part(give, 1 - core, chunk(m), BLOCK - EARLY[m][0], a, d, None)
+            swap_part(m, n).start()
+
+    def release(m):
+        for n, (a, d) in enumerate(remote):
+            swap_part(m, n).wait_recv()
+            part(canvas, core, chunk(m), BLOCK - EARLY[m][0], a, d, take)
+            first_copy(m, a, d).start()
+
+    def home(target, which, extra):
+        for a in range(2):
+            if extra is not None:
+                swap_home(a).wait_recv()
+            for start in range(0, BLOCK, STEP):
+                part(target, which, pl.ds(sky_rows - BLOCK + start, STEP), start, a, 0, extra)
+            if extra is None:
+                swap_home(a).start()
+
     def build(m, sky_block, start, last=False):
-        if isinstance(m, int) and m < FINE:
-            for a, d in order():
-                part(give, 1 - core, m, sky_block, start, a, d, None)
-            return
-        one = cover(give, 1 - core, m, sky_block, start, (0, 1), lambda n: n, last, None)
+        one = cover(give, 1 - core, chunk(m), sky_block, start, (0, 1), lambda n: n, last, None)
         lax.fori_loop(0, ny * nx, one, 0)
-        swap(m).start()
-
-    def offer(m):
-        for a, d in order():
-            swap(m, a, d).start()
+        swap_all(m).start()
 
     def combine(m, sky_block, start, last=False):
-        if isinstance(m, int) and m < FINE:
-            for a, d in order():
-                swap(m, a, d).wait_recv()
-                part(canvas, core, m, sky_block, start, a, d, take)
-                if d:
-                    first_copy(m, a, d).start()
-            return
-        swap(m).wait_recv()
-        one = cover(canvas, core, m, sky_block, start, (0, 1), lambda n: n, last, take)
+        swap_all(m).wait_recv()
+        one = cover(canvas, core, chunk(m), sky_block, start, (0, 1), lambda n: n, last, take)
         lax.fori_loop(0, ny * nx, one, 0)
-        for a, d in order():
-            if d:
-                first_copy(m, a, d).start()
+        for a, d in remote:
+            first_copy(m, a, d).start()
 
     halo = pltpu.make_async_remote_copy(
         halo_out, halo_in, halo_sem.at[0], halo_sem.at[1],
@@ -303,13 +318,11 @@
             halo_out[a, sky_tile] = sum_rows(a, top_terms, index, BLOCK, 8)
         return 0
 
+    bottom = blocks - 1
     loaded(0)
-    interpolate(blocks - 1, BLOCK - READY, BLOCK)
-    build(0, top, BLOCK - START)
+    interpolate(bottom, 104, 128, 3)
     pl.semaphore_wait(barrier, len(near) + jnp.where(tile > 0, 1, 0))
-    offer(0)
-    loaded(1)
-    interpolate(blocks - 1, 0, BLOCK - READY)
+    begin(0)
 
     @pl.when(tile > 0)
     def _():
@@ -319,14 +332,27 @@
     def _():
         halo_in[...] = jnp.zeros(halo_in.shape, F32)
 
-    combine(0, top, BLOCK - START)
-    build(1, top, START)
-    offer(1)
+    loaded(1)
+    interpolate(bottom, 88, 104, 2)
+    begin(1)
+    release(0)
+    loaded(2)
+    interpolate(bottom, 56, 88, 4)
+    release(1)
+    begin(2)
+    interpolate(bottom, 0, 56, 7)
+    release(2)
     for k, b in enumerate(reversed(range(blocks - 1))):
-        loaded(2 + k)
-        interpolate(b, 0, BLOCK)
-    combine(1, top, START)
-    build(2, top, 0)
+        loaded(len(PIECES) + k)
+        interpolate(b, 112, 128, 2)
+    begin(3)
+    for b in reversed(range(blocks - 1)):
+        interpolate(b, 40, 112, 3)
+    release(3)
+    for b in reversed(range(blocks - 1)):
+        interpolate(b, 0, 40, 5)
+    build(FINE, top - 1, STEP)
+    home(give, 1 - core, None)
     lax.fori_loop(0, sky_tiles, border, 0, unroll=4)
 
     @pl.when(tile < n_tile - 1)
@@ -334,15 +360,12 @@
         pl.semaphore_wait(entered, 1)
         halo.start()
 
-    build(3, top - 1, STEP)
-    combine(2, top, 0)
-
     def spread(i, _):
         at = top - 1 - i
-        build(4 + 2 * i, at, 0)
-        combine(3 + 2 * i, at, STEP)
-        build(5 + 2 * i, at - 1, STEP)
-        combine(4 + 2 * i, at, 0)
+        build(FINE + 1 + 2 * i, at, 0)
+        combine(FINE + 2 * i, at, STEP)
+        build(FINE + 2 + 2 * i, at - 1, STEP)
+        combine(FINE + 1 + 2 * i, at, 0)
         return 0
 
     lax.fori_loop(0, top - 1, spread, 0)
@@ -354,6 +377,7 @@
     build(chunks - 1, 0, 0, last=True)
     combine(chunks - 2, 0, STEP)
     combine(chunks - 1, 0, 0, last=True)
+    home(canvas, core, take)
 
     def every(step):
         for m in range(len(EARLY)):
@@ -367,17 +391,17 @@
 
     def middle(m):
         rows = chunk(m)
+        arrived(inbox.at[pl.ds(0, first_tiles), rows], first_sem.at[m])
         for a in range(2):
-            arrived(firsts[a].at[:, :, rows], first_sem.at[m, a])
-            first, _ = block_of(a, 0)
             for e in range(1, counts[1 - a]):
-                at = lax.rem(places[1 - a] + e, counts[1 - a]) * half
+                at = place_of(1 - a, e) * half
 
                 def one(q, _):
-                    total = canvas[a, first + at + q, rows]
+                    slot = place_of(a, 0) * sizes[a] + at + q
+                    total = canvas[a, slot, rows]
                     for d in range(counts[a] - 1):
-                        total = total + firsts[a][d, at + q, rows]
-                    canvas[a, first + at + q, rows] = total
+                        total = total + inbox[offsets[a] + d * sizes[a] + at + q, rows]
+                    canvas[a, slot, rows] = total
                     return 0
 
                 lax.fori_loop(0, half, one, 0, unroll=True)
@@ -387,17 +411,16 @@
 
     def finish(m):
         rows = chunk(m)
-        arrived(second.at[:, :, rows], second_sem.at[m])
+        arrived(inbox.at[pl.ds(first_tiles, every_tile - first_tiles), rows], second_sem.at[m])
         for q in range(half):
             sums = []
             for a in range(2):
-                first, _ = block_of(a, 0)
                 at = places[1 - a] * half + q
-                total = canvas[a, first + at, rows]
+                total = canvas[a, place_of(a, 0) * sizes[a] + at, rows]
                 for d in range(counts[a] - 1):
-                    total = total + firsts[a][d, at, rows]
+                    total = total + inbox[offsets[a] + d * sizes[a] + at, rows]
                 for e in range(counts[1 - a] - 1):
-                    total = total + seconds[a][e, q, rows]
+                    total = total + inbox[second_tiles[a] + e * half + q, rows]
                 sums.append(total)
             lanes = slice(q * LANES, (q + 1) * LANES)
             numer[rows, lanes] = sums[0]
@@ -405,11 +428,8 @@
             normalised[rows, lanes] = sums[0] / jnp.maximum(sums[1], 0.05)
 
     every(finish)
-
     arrived(give, send_sem.at[0])
-    for a in range(2):
-        arrived(firsts[a], send_sem.at[1 + a])
-        arrived(seconds[a], send_sem.at[3 + a])
+    arrived(inbox, send_sem.at[1])
 
     @pl.when(tile < n_tile - 1)
     def _():
@@ -435,7 +455,7 @@
     per_core = sky_tiles // 2
     chunks = len(EARLY) + (TILE_BLOCKS - 1) * (BLOCK // STEP)
     own_cols = half * LANES
-    most = max(nx, ny)
+    inbox_tiles = (nx - 1) * (ny + 1) * half + (ny - 1) * (nx + 1) * half
     dma = pltpu.SemaphoreType.DMA
     anywhere = pl.BlockSpec(memory_space=pl.ANY)
     scalars = [pltpu.SMEM(v.shape, v.dtype) for v in (row_block, col_block, band, row_frac, col_frac)]
@@ -454,17 +474,15 @@
             pltpu.VMEM((2, per_core, sky_rows, LANES), F32),
             pltpu.VMEM((2, per_core, sky_rows, LANES), F32),
             pltpu.VMEM((2, per_core, sky_rows, LANES), F32),
-            pltpu.VMEM((nx - 1, ny * half, sky_rows, LANES), F32),
-            pltpu.VMEM((ny - 1, nx * half, sky_rows, LANES), F32),
-            pltpu.VMEM((ny - 1 + nx - 1, half, sky_rows, LANES), F32),
+            pltpu.VMEM((inbox_tiles, sky_rows, LANES), F32),
             dma((5,)),
-            dma((blocks + 1,)),
+            dma((len(PIECES) + blocks - 1,)),
             dma((2,)),
             pltpu.SemaphoreType.REGULAR,
-            dma((chunks + FINE * (2 * most - 1),)),
-            dma((chunks, 2)),
+            dma((FINE * (nx + ny - 2) + 2 + chunks - FINE,)),
             dma((chunks,)),
-            dma((5,)),
+            dma((chunks,)),
+            dma((2,)),
         ],
         compiler_params=pltpu.CompilerParams(
             collective_id=0, has_side_effects=True, vmem_limit_bytes=56 * 1024 * 1024

time: 78.7 us -> 77.2 us (0.981)
  Pallas kernels: 77.9 us -> 76.4 us
    pallas_call x1, Pallas kernels: 76.2 us -> 74.7 us  [body(): pl.pallas_call(functools.partial(kernel, ny, nx, n_tile), out_shape=(out,...]
where the time goes in v3:
time: 77.2 us; the launch traced here: 77.1 us
  Pallas kernels  76.4 us (99%)
    pallas_call x1, Pallas kernels, body(): pl.pallas_call(functools.partial(kernel, ny, nx, n_tile), out_shape=(out,...  74.7 us
    pallas_call x1, Pallas kernels, body(): pl.pallas_call(copy_out, out_shape=(flat, flat, flat), in_specs=[vmem] *...  1.69 us

profile of v3, /device:TPU:0, one launch (start us, length us, event | category | flops | bytes accessed | tf_op | source)
XLA Modules:
  0.0 77.1 jit_solution(3480076103687194820)
XLA Ops:
  0.6 74.7 %combine.1 = (f32[512,512]{1,0:T(8,128)S(1)}, f32[512,512]{1,0:T(8,128)S(1)}, f32[512,512]{1,0:T(8,128)S(1)}) custom-call(f32[2,256,2048]{2,1,0:T(8,128)} %images.1, f32[2,256,2048]{2,1,0:T(8,128)} %beams.1, s32[2]{0:T(128)} %row_block_in.1, s32[2]{0:T(128)} %col_block_in.1, s32[2,2]{1,0:T(2,128)} %band_in.1, f32[2]{0:T(128)} %row_frac_in.1, f32[2]{0:T(128)} %col_frac_in.1), custom_call_target="tpu_custom_call" | custom-call | tf_op jit(solution)/shard_map/combine/pallas_call | solution.py:464
  75.4 1.7 %copy_out.1 = (f32[512,512]{1,0:T(8,128)}, f32[512,512]{1,0:T(8,128)}, f32[512,512]{1,0:T(8,128)}) custom-call(f32[512,512]{1,0:T(8,128)S(1)} %get-tuple-element.6.numer, f32[512,512]{1,0:T(8,128)S(1)} %get-tuple-element.7.weight, f32[512,512]{1,0:T(8,128)S(1)} %get-tuple-element.8.normalised), custom_call_target="tpu_custom_call" | custom-call | tf_op jit(solution)/shard_map/copy_out/pallas_call | solution.py:493

commit v4 on v3

--- a/solution.py
+++ b/solution.py
@@ -16,9 +16,10 @@
 STEP = 64
 START = 32
 READY = START + PAD
-PIECES = ((104, 128), (88, 104), (0, 88))
-EARLY = ((16, 16), (32, 16), (64, 32), (BLOCK, STEP))
+PIECES = ((104, 128), (80, 104), (0, 80))
+EARLY = ((16, 16), (40, 24), (64, 24), (BLOCK, STEP))
 FINE = len(EARLY)
+DETOUR = 1
 MESH = pl.DeviceIdType.MESH
 F32 = jnp.float32
 
@@ -37,8 +38,8 @@
     numer, weight, normalised,
     row_block, col_block, band, row_frac, col_frac,
     raw, shaped, halo_out, halo_in, give, take, canvas,
-    inbox,
-    small_sem, load_sem, halo_sem, entered, swap_sem, first_sem, second_sem, send_sem,
+    inbox, detour,
+    small_sem, load_sem, halo_sem, entered, swap_sem, first_sem, second_sem, send_sem, detour_sem,
 ):
     points, img_rows, width = images.shape
     blocks = img_rows // BLOCK
@@ -233,6 +234,51 @@
             device_id={"pgroup": peers[1 - a][d - 1]}, device_id_type=MESH,
         )
 
+    square = nx == 2 and ny == 2
+
+    def at_corner(a, first, second):
+        return (places[a] == first) & (places[1 - a] == second)
+
+    def short_copy(a):
+        rows = chunk(DETOUR)
+        return pltpu.make_async_remote_copy(
+            canvas.at[a, pl.ds(0, half), rows], inbox.at[pl.ds(offsets[a], half), rows],
+            send_sem.at[1], first_sem.at[DETOUR],
+            device_id={"pgroup": peers[a][0]}, device_id_type=MESH,
+        )
+
+    def detour_copy(a):
+        return pltpu.make_async_remote_copy(
+            canvas.at[a, pl.ds(half, half), chunk(DETOUR)], detour.at[a],
+            send_sem.at[1], detour_sem.at[a],
+            device_id={"pgroup": peers[1 - a][0]}, device_id_type=MESH,
+        )
+
+    def late_copy(a):
+        rows = chunk(DETOUR)
+        return pltpu.make_async_remote_copy(
+            canvas.at[a, pl.ds(half, half), rows], inbox.at[pl.ds(offsets[a] + half, half), rows],
+            send_sem.at[1], second_sem.at[DETOUR],
+            device_id={"pgroup": peers[a][0]}, device_id_type=MESH,
+        )
+
+    def send_first(m, a, d):
+        if not (square and isinstance(m, int) and m == DETOUR):
+            first_copy(m, a, d).start()
+            return
+
+        @pl.when(places[a] == 0)
+        def _():
+            first_copy(m, a, d).start()
+
+        @pl.when(places[a] == 1)
+        def _():
+            short_copy(a).start()
+
+        @pl.when(at_corner(a, 1, 0))
+        def _():
+            detour_copy(a).start()
+
     def arrived(view, sem):
         pltpu.make_async_copy(view, view, sem).wait()
 
@@ -281,7 +327,7 @@
         for n, (a, d) in enumerate(remote):
             swap_part(m, n).wait_recv()
             part(canvas, core, chunk(m), BLOCK - EARLY[m][0], a, d, take)
-            first_copy(m, a, d).start()
+            send_first(m, a, d)
 
     def home(target, which, extra):
         for a in range(2):
@@ -333,11 +379,11 @@
         halo_in[...] = jnp.zeros(halo_in.shape, F32)
 
     loaded(1)
-    interpolate(bottom, 88, 104, 2)
+    interpolate(bottom, 80, 104, 3)
     begin(1)
     release(0)
     loaded(2)
-    interpolate(bottom, 56, 88, 4)
+    interpolate(bottom, 56, 80, 3)
     release(1)
     begin(2)
     interpolate(bottom, 0, 56, 7)
@@ -391,7 +437,14 @@
 
     def middle(m):
         rows = chunk(m)
-        arrived(inbox.at[pl.ds(0, first_tiles), rows], first_sem.at[m])
+        bent = square and isinstance(m, int) and m == DETOUR
+        if bent:
+            for n in range(3):
+                @pl.when(x + y == n)
+                def _():
+                    arrived(inbox.at[pl.ds(0, (2 + n) * half), rows], first_sem.at[m])
+        else:
+            arrived(inbox.at[pl.ds(0, first_tiles), rows], first_sem.at[m])
         for a in range(2):
             for e in range(1, counts[1 - a]):
                 at = place_of(1 - a, e) * half
@@ -404,14 +457,36 @@
                     canvas[a, slot, rows] = total
                     return 0
 
-                lax.fori_loop(0, half, one, 0, unroll=True)
+                if bent:
+                    @pl.when(~at_corner(a, 0, 0))
+                    def _():
+                        lax.fori_loop(0, half, one, 0, unroll=True)
+                else:
+                    lax.fori_loop(0, half, one, 0, unroll=True)
                 second_copy(m, a, e).start()
+            if bent:
+                @pl.when(at_corner(a, 1, 1))
+                def _():
+                    arrived(detour.at[a], detour_sem.at[a])
+                    for q in range(half):
+                        canvas[a, half + q, rows] += detour[a, q]
+                    late_copy(a).start()
 
     every(middle)
 
     def finish(m):
         rows = chunk(m)
-        arrived(inbox.at[pl.ds(first_tiles, every_tile - first_tiles), rows], second_sem.at[m])
+        second_count = every_tile - first_tiles
+        if square and isinstance(m, int) and m == DETOUR:
+            @pl.when(x == y)
+            def _():
+                arrived(inbox.at[pl.ds(0, second_count), rows], second_sem.at[m])
+
+            @pl.when(x != y)
+            def _():
+                arrived(inbox.at[pl.ds(0, second_count + half), rows], second_sem.at[m])
+        else:
+            arrived(inbox.at[pl.ds(first_tiles, second_count), rows], second_sem.at[m])
         for q in range(half):
             sums = []
             for a in range(2):
@@ -475,6 +550,7 @@
             pltpu.VMEM((2, per_core, sky_rows, LANES), F32),
             pltpu.VMEM((2, per_core, sky_rows, LANES), F32),
             pltpu.VMEM((inbox_tiles, sky_rows, LANES), F32),
+            pltpu.VMEM((2, half, EARLY[DETOUR][1], LANES), F32),
             dma((5,)),
             dma((len(PIECES) + blocks - 1,)),
             dma((2,)),
@@ -482,6 +558,7 @@
             dma((FINE * (nx + ny - 2) + 2 + chunks - FINE,)),
             dma((chunks,)),
             dma((chunks,)),
+            dma((2,)),
             dma((2,)),
         ],
         compiler_params=pltpu.CompilerParams(

time: 77.2 us -> 76.2 us (0.987)
  Pallas kernels: 76.4 us -> 75.4 us
    pallas_call x1, Pallas kernels: 74.7 us -> 73.7 us  [body(): pl.pallas_call(functools.partial(kernel, ny, nx, n_tile), out_shape=(out,...]
where the time goes in v4:
time: 76.2 us; the launch traced here: 76 us
  Pallas kernels  75.4 us (99%)
    pallas_call x1, Pallas kernels, body(): pl.pallas_call(functools.partial(kernel, ny, nx, n_tile), out_shape=(out,...  73.7 us
    pallas_call x1, Pallas kernels, body(): pl.pallas_call(copy_out, out_shape=(flat, flat, flat), in_specs=[vmem] *...  1.69 us

profile of v4, /device:TPU:0, one launch (start us, length us, event | category | flops | bytes accessed | tf_op | source)
XLA Modules:
  0.0 76.0 jit_solution(10453724407220612262)
XLA Ops:
  0.6 73.7 %combine.1 = (f32[512,512]{1,0:T(8,128)S(1)}, f32[512,512]{1,0:T(8,128)S(1)}, f32[512,512]{1,0:T(8,128)S(1)}) custom-call(f32[2,256,2048]{2,1,0:T(8,128)} %images.1, f32[2,256,2048]{2,1,0:T(8,128)} %beams.1, s32[2]{0:T(128)} %row_block_in.1, s32[2]{0:T(128)} %col_block_in.1, s32[2,2]{1,0:T(2,128)} %band_in.1, f32[2]{0:T(128)} %row_frac_in.1, f32[2]{0:T(128)} %col_frac_in.1), custom_call_target="tpu_custom_call" | custom-call | tf_op jit(solution)/shard_map/combine/pallas_call | solution.py:539
  74.4 1.7 %copy_out.1 = (f32[512,512]{1,0:T(8,128)}, f32[512,512]{1,0:T(8,128)}, f32[512,512]{1,0:T(8,128)}) custom-call(f32[512,512]{1,0:T(8,128)S(1)} %get-tuple-element.6.numer, f32[512,512]{1,0:T(8,128)S(1)} %get-tuple-element.7.weight, f32[512,512]{1,0:T(8,128)S(1)} %get-tuple-element.8.normalised), custom_call_target="tpu_custom_call" | custom-call | tf_op jit(solution)/shard_map/copy_out/pallas_call | solution.py:570

commit v5 on v4

--- a/solution.py
+++ b/solution.py
@@ -20,6 +20,7 @@
 EARLY = ((16, 16), (40, 24), (64, 24), (BLOCK, STEP))
 FINE = len(EARLY)
 DETOUR = 1
+GROUPS = ((0, 2, 3), (DETOUR,), (4, 5), (6, 7), (8,), (9,))
 MESH = pl.DeviceIdType.MESH
 F32 = jnp.float32
 
@@ -80,10 +81,12 @@
         low, size = pieces[k]
         for p in range(points):
             for which, source in enumerate((images, beams)):
-                rows = pl.ds(low, size)
-                pltpu.make_async_copy(
-                    source.at[p, rows], raw.at[which, p, rows], load_sem.at[k]
-                ).start()
+                step = 8 if k == 0 else size
+                for at in range(low, low + size, step):
+                    rows = pl.ds(at, step)
+                    pltpu.make_async_copy(
+                        source.at[p, rows], raw.at[which, p, rows], load_sem.at[k]
+                    ).start()
 
     load(0)
     small = [
@@ -198,29 +201,41 @@
         start = sky_rows - BLOCK - STEP * (m - len(EARLY) + 1)
         return pl.ds(pl.multiple_of(start, STEP), STEP)
 
+    def group_of(m):
+        return [m in group for group in GROUPS].index(True)
+
+    def group_rows(m):
+        return pl.ds(0, sum(chunk(n).size for n in GROUPS[group_of(m)]))
+
+    def opens(m):
+        return GROUPS[group_of(m)][0] == m
+
     def swap(view, sem):
         return pltpu.make_async_remote_copy(
             give.at[view], take.at[view], send_sem.at[0], swap_sem.at[sem],
             device_id={"pgroup": partner}, device_id_type=MESH,
         )
 
+    parts = len(remote)
+    parts_tiles = sum(sizes[a] for a, _ in remote) // 2
+
     def swap_part(m, n):
         a, d = remote[n]
-        return swap((a, block_of(a, d), chunk(m)), m * len(remote) + n)
+        return swap((a, block_of(a, d), chunk(m)), n if m == 0 else parts + m - 1)
 
     def swap_home(a):
         rows = pl.ds(sky_rows - BLOCK, BLOCK)
-        return swap((a, block_of(a, 0), rows), FINE * len(remote) + a)
+        return swap((a, block_of(a, 0), rows), parts + FINE - 1)
 
     def swap_all(m):
-        return swap((slice(None), slice(None), chunk(m)), FINE * len(remote) + 2 + m - FINE)
+        return swap((slice(None), slice(None), chunk(m)), parts + m)
 
     def first_copy(m, a, d):
         rows = chunk(m)
         at = pl.ds(offsets[a] + (d - 1) * sizes[a], sizes[a])
         return pltpu.make_async_remote_copy(
             canvas.at[a, block_of(a, d), rows], inbox.at[at, rows],
-            send_sem.at[1], first_sem.at[m],
+            send_sem.at[1], first_sem.at[group_of(m)],
             device_id={"pgroup": peers[a][d - 1]}, device_id_type=MESH,
         )
 
@@ -230,7 +245,7 @@
         at = pl.ds(second_tiles[a] + (d - 1) * half, half)
         return pltpu.make_async_remote_copy(
             canvas.at[a, pl.ds(source, half), rows], inbox.at[at, rows],
-            send_sem.at[1], second_sem.at[m],
+            send_sem.at[1], second_sem.at[group_of(m)],
             device_id={"pgroup": peers[1 - a][d - 1]}, device_id_type=MESH,
         )
 
@@ -243,7 +258,7 @@
         rows = chunk(DETOUR)
         return pltpu.make_async_remote_copy(
             canvas.at[a, pl.ds(0, half), rows], inbox.at[pl.ds(offsets[a], half), rows],
-            send_sem.at[1], first_sem.at[DETOUR],
+            send_sem.at[1], first_sem.at[group_of(DETOUR)],
             device_id={"pgroup": peers[a][0]}, device_id_type=MESH,
         )
 
@@ -258,7 +273,7 @@
         rows = chunk(DETOUR)
         return pltpu.make_async_remote_copy(
             canvas.at[a, pl.ds(half, half), rows], inbox.at[pl.ds(offsets[a] + half, half), rows],
-            send_sem.at[1], second_sem.at[DETOUR],
+            send_sem.at[1], second_sem.at[group_of(DETOUR)],
             device_id={"pgroup": peers[a][0]}, device_id_type=MESH,
         )
 
@@ -324,15 +339,19 @@
             swap_part(m, n).start()
 
     def release(m):
+        if m:
+            arrived(take.at[:, pl.ds(0, parts_tiles), chunk(m)], swap_sem.at[parts + m - 1])
         for n, (a, d) in enumerate(remote):
-            swap_part(m, n).wait_recv()
+            if m == 0:
+                swap_part(m, n).wait_recv()
             part(canvas, core, chunk(m), BLOCK - EARLY[m][0], a, d, take)
             send_first(m, a, d)
 
     def home(target, which, extra):
+        if extra is not None:
+            both = pl.ds(0, (sizes[0] + sizes[1]) // 2)
+            arrived(take.at[:, both, pl.ds(sky_rows - BLOCK, BLOCK)], swap_sem.at[parts + FINE - 1])
         for a in range(2):
-            if extra is not None:
-                swap_home(a).wait_recv()
             for start in range(0, BLOCK, STEP):
                 part(target, which, pl.ds(sky_rows - BLOCK + start, STEP), start, a, 0, extra)
             if extra is None:
@@ -406,15 +425,12 @@
         pl.semaphore_wait(entered, 1)
         halo.start()
 
-    def spread(i, _):
+    for i in range(top - 1):
         at = top - 1 - i
         build(FINE + 1 + 2 * i, at, 0)
         combine(FINE + 2 * i, at, STEP)
         build(FINE + 2 + 2 * i, at - 1, STEP)
         combine(FINE + 1 + 2 * i, at, 0)
-        return 0
-
-    lax.fori_loop(0, top - 1, spread, 0)
 
     @pl.when(tile > 0)
     def _():
@@ -426,25 +442,19 @@
     home(canvas, core, take)
 
     def every(step):
-        for m in range(len(EARLY)):
+        for m in range(chunks):
             step(m)
-
-        def one(m, _):
-            step(m)
-            return 0
-
-        lax.fori_loop(len(EARLY), chunks, one, 0)
 
     def middle(m):
         rows = chunk(m)
-        bent = square and isinstance(m, int) and m == DETOUR
+        bent = square and m == DETOUR
         if bent:
             for n in range(3):
                 @pl.when(x + y == n)
                 def _():
-                    arrived(inbox.at[pl.ds(0, (2 + n) * half), rows], first_sem.at[m])
-        else:
-            arrived(inbox.at[pl.ds(0, first_tiles), rows], first_sem.at[m])
+                    arrived(inbox.at[pl.ds(0, (2 + n) * half), rows], first_sem.at[group_of(m)])
+        elif opens(m):
+            arrived(inbox.at[pl.ds(0, first_tiles), group_rows(m)], first_sem.at[group_of(m)])
         for a in range(2):
             for e in range(1, counts[1 - a]):
                 at = place_of(1 - a, e) * half
@@ -477,16 +487,16 @@
     def finish(m):
         rows = chunk(m)
         second_count = every_tile - first_tiles
-        if square and isinstance(m, int) and m == DETOUR:
+        if square and m == DETOUR:
             @pl.when(x == y)
             def _():
-                arrived(inbox.at[pl.ds(0, second_count), rows], second_sem.at[m])
+                arrived(inbox.at[pl.ds(0, second_count), rows], second_sem.at[group_of(m)])
 
             @pl.when(x != y)
             def _():
-                arrived(inbox.at[pl.ds(0, second_count + half), rows], second_sem.at[m])
-        else:
-            arrived(inbox.at[pl.ds(first_tiles, second_count), rows], second_sem.at[m])
+                arrived(inbox.at[pl.ds(0, second_count + half), rows], second_sem.at[group_of(m)])
+        elif opens(m):
+            arrived(inbox.at[pl.ds(first_tiles, second_count), group_rows(m)], second_sem.at[group_of(m)])
         for q in range(half):
             sums = []
             for a in range(2):
@@ -555,9 +565,9 @@
             dma((len(PIECES) + blocks - 1,)),
             dma((2,)),
             pltpu.SemaphoreType.REGULAR,
-            dma((FINE * (nx + ny - 2) + 2 + chunks - FINE,)),
-            dma((chunks,)),
-            dma((chunks,)),
+            dma((nx + ny - 2 + chunks,)),
+            dma((len(GROUPS),)),
+            dma((len(GROUPS),)),
             dma((2,)),
             dma((2,)),
         ],

time: 76.2 us -> 76.1 us (level)
  no operation moved by 1% of the time
where the time goes in v5:
time: 76.1 us; the launch traced here: 76 us
  Pallas kernels  75.3 us (99%)
    pallas_call x1, Pallas kernels, body(): pl.pallas_call(functools.partial(kernel, ny, nx, n_tile), out_shape=(out,...  73.7 us
    pallas_call x1, Pallas kernels, body(): pl.pallas_call(copy_out, out_shape=(flat, flat, flat), in_specs=[vmem] *...  1.69 us

profile of v5, /device:TPU:0, one launch (start us, length us, event | category | flops | bytes accessed | tf_op | source)
XLA Modules:
  0.0 76.0 jit_solution(10307584032475341044)
XLA Ops:
  0.6 73.7 %combine.1 = (f32[512,512]{1,0:T(8,128)S(1)}, f32[512,512]{1,0:T(8,128)S(1)}, f32[512,512]{1,0:T(8,128)S(1)}) custom-call(f32[2,256,2048]{2,1,0:T(8,128)} %images.1, f32[2,256,2048]{2,1,0:T(8,128)} %beams.1, s32[2]{0:T(128)} %row_block_in.1, s32[2]{0:T(128)} %col_block_in.1, s32[2,2]{1,0:T(2,128)} %band_in.1, f32[2]{0:T(128)} %row_frac_in.1, f32[2]{0:T(128)} %col_frac_in.1), custom_call_target="tpu_custom_call" | custom-call | tf_op jit(solution)/shard_map/combine/pallas_call | solution.py:549
  74.3 1.7 %copy_out.1 = (f32[512,512]{1,0:T(8,128)}, f32[512,512]{1,0:T(8,128)}, f32[512,512]{1,0:T(8,128)}) custom-call(f32[512,512]{1,0:T(8,128)S(1)} %get-tuple-element.6.numer, f32[512,512]{1,0:T(8,128)S(1)} %get-tuple-element.7.weight, f32[512,512]{1,0:T(8,128)S(1)} %get-tuple-element.8.normalised), custom_call_target="tpu_custom_call" | custom-call | tf_op jit(solution)/shard_map/copy_out/pallas_call | solution.py:580
